TPU v7x, 32 devices: a whole 2x2x4 slice. The times are simulated.
32 devices in a mesh: dp: 8 (over y, x, core), expert: 4 (over z).
Axes of the slice: x: 2, y: 2, z: 4, core: 2. Of those that a mesh axis runs over, the one named last changes fastest.
Arguments:
- tokens: bfloat16 [4096, 2048], P(('dp', 'expert')), may hold values from -6 to 6
- cotangent: bfloat16 [4096, 2048], P(('dp', 'expert')), may hold values from -6 to 6
- expert_ids: int32 [4096, 2], P(('dp', 'expert')), may hold values from 0 to 3, all different within a row; in each aligned block of 128 rows (0 to 127, 128 to 255, ...) at most 128 rows name the same one
- combine: float32 [4096, 2], P(('dp', 'expert')), may hold values from 0.1 to 1
- w_gate: bfloat16 [4, 2048, 768], P('expert'), may hold values from -0.125 to 0.125
- w_up: bfloat16 [4, 2048, 768], P('expert'), may hold values from -0.125 to 0.125
- w_down: bfloat16 [4, 768, 2048], P('expert'), may hold values from -0.21875 to 0.21875
Outputs:
- input_grad: bfloat16 [4096, 2048], P(('dp', 'expert'))
- combine_grad: float32 [4096, 2], P(('dp', 'expert'))
- gate_grad: bfloat16 [4, 2048, 768], P('expert', 'dp')
- up_grad: bfloat16 [4, 2048, 768], P('expert', 'dp')
- down_grad: bfloat16 [4, 768, 2048], P('expert', 'dp')
Inputs may be any that keep to these rules, and one draw needn't show every extreme that they name: `expert_ids`: each token names 2 different experts. In the rows of one device no expert is named by more than 128 tokens, and in some devices' rows some expert is named by exactly 128.
All inputs are finite; a program needn't handle non-finite values.
Results may differ from a plain program's by a relative error of at most 0.02.
Values may be sent and summed in bfloat16 or wider, within the bound.
A program may use at most 128 MiB of HBM per device.

v0:
```python
import jax
import jax.numpy as jnp
from jax import lax
from jax.sharding import PartitionSpec as P


def slot_table(expert_ids, experts_all, capacity):
    pairs = expert_ids.reshape(-1)
    count = pairs.shape[0]
    onehot = (pairs[:, None] == jnp.arange(experts_all, dtype=jnp.int32)[None, :]).astype(jnp.int32)
    before = jnp.cumsum(onehot, axis=0) - onehot
    position = jnp.sum(before * onehot, axis=1)
    dest = pairs * capacity + position
    filled = (
        jnp.zeros((experts_all * capacity,), jnp.int32)
        .at[dest]
        .set(jnp.arange(count, dtype=jnp.int32) + 1)
    )
    return (dest, filled)


def gather_rows(tokens, cotangent, combine, filled, top):
    live = filled > 0
    pair = jnp.maximum(filled - 1, 0)
    source = pair // top
    rows_x = jnp.where(live[:, None], jnp.take(tokens, source, axis=0), jnp.zeros((), tokens.dtype))
    rows_dy = jnp.where(
        live[:, None], jnp.take(cotangent, source, axis=0), jnp.zeros((), cotangent.dtype)
    )
    rows_c = jnp.where(
        live, jnp.take(combine.reshape(-1), pair, axis=0), jnp.zeros((), combine.dtype)
    )
    return (rows_x, rows_dy, rows_c)


def forward_part(rows_x, gate_mat, up_mat, down_mat):
    gate = jnp.dot(rows_x, gate_mat, preferred_element_type=jnp.float32)
    up = jnp.dot(rows_x, up_mat, preferred_element_type=jnp.float32)
    sig = jax.nn.sigmoid(gate)
    act = gate * sig
    hidden = (act * up).astype(jnp.bfloat16)
    output = jnp.dot(hidden, down_mat, preferred_element_type=jnp.float32)
    return (gate, up, sig, act, hidden, output)


def backward_part(state, rows_dy, rows_c, gate_mat, up_mat, down_mat):
    gate, up, sig, act, hidden, output = state
    comb_grad = jnp.sum(rows_dy.astype(jnp.float32) * output, axis=1)
    scaled = (rows_c[:, None] * rows_dy.astype(jnp.float32)).astype(jnp.bfloat16)
    last = (((1,), (1,)), ((), ()))
    hidden_grad = lax.dot_general(scaled, down_mat, last, preferred_element_type=jnp.float32)
    gate_d = (hidden_grad * up * (sig * (1.0 + gate * (1.0 - sig)))).astype(jnp.bfloat16)
    up_d = (hidden_grad * act).astype(jnp.bfloat16)
    row_grad = lax.dot_general(gate_d, gate_mat, last, preferred_element_type=jnp.float32)
    row_grad = (
        row_grad + lax.dot_general(up_d, up_mat, last, preferred_element_type=jnp.float32)
    ).astype(jnp.bfloat16)
    return (comb_grad, scaled, gate_d, up_d, row_grad)


def shards(tokens, cotangent, expert_ids, combine, w_gate, w_up, w_down):
    first = (((0,), (0,)), ((), ()))
    local_experts = w_gate.shape[0]
    groups = lax.axis_size("expert")
    replicas = lax.axis_size("dp")
    experts_all = local_experts * groups
    tok_rows, top = expert_ids.shape
    feature = tokens.shape[1]
    hidden_width = w_gate.shape[2]
    capacity = 2 * tok_rows * top // experts_all
    dest, filled = slot_table(expert_ids, experts_all, capacity)
    rows_x, rows_dy, rows_c = gather_rows(tokens, cotangent, combine, filled, top)
    rows_x = rows_x.reshape(experts_all, capacity, feature)
    rows_dy = rows_dy.reshape(experts_all, capacity, feature)
    rows_c = rows_c.reshape(experts_all, capacity)
    recv_x, recv_dy, recv_c = (
        lax.all_to_all(rows_x, "expert", split_axis=0, concat_axis=1, tiled=True),
        lax.all_to_all(rows_dy, "expert", split_axis=0, concat_axis=1, tiled=True),
        lax.all_to_all(
            rows_c.astype(jnp.bfloat16), "expert", split_axis=0, concat_axis=1, tiled=True
        ).astype(rows_c.dtype),
    )
    states = forward_part(recv_x[0], w_gate[0], w_up[0], w_down[0])
    comb_grad, scaled, gate_d, up_d, row_grad = backward_part(
        states, recv_dy[0], recv_c[0], w_gate[0], w_up[0], w_down[0]
    )
    row_list = [row_grad]
    comb_list = [comb_grad]
    inputs = recv_x[0]
    hidden = states[4]
    paired = jnp.concatenate([gate_d, up_d], axis=1)

    def gate_up_term(start, count, inputs=inputs, paired=paired):
        return lax.dot_general(inputs, paired, first, preferred_element_type=jnp.float32)

    def down_term(start, count, hidden=hidden, scaled=scaled):
        return lax.dot_general(hidden, scaled, first, preferred_element_type=jnp.float32)

    both = lax.psum_scatter(
        gate_up_term(jnp.int32(0), feature // replicas * lax.axis_size("dp")).astype(jnp.bfloat16),
        "dp",
        scatter_dimension=0,
        tiled=True,
    ).astype(jnp.float32)
    gate_terms = [both[:, :hidden_width].astype(jnp.bfloat16)]
    up_terms = [both[:, hidden_width:].astype(jnp.bfloat16)]
    down_sum = lax.psum_scatter(
        down_term(jnp.int32(0), hidden_width // replicas * lax.axis_size("dp")).astype(
            jnp.bfloat16
        ),
        "dp",
        scatter_dimension=0,
        tiled=True,
    )
    down_terms = [down_sum]
    gate_grad = jnp.stack(gate_terms)
    up_grad = jnp.stack(up_terms)
    down_grad = jnp.stack(down_terms)
    back_rows, back_comb = (
        lax.all_to_all(jnp.stack(row_list), "expert", split_axis=1, concat_axis=0, tiled=True),
        lax.all_to_all(
            jnp.stack(comb_list).astype(jnp.bfloat16),
            "expert",
            split_axis=1,
            concat_axis=0,
            tiled=True,
        ).astype(jnp.float32),
    )
    flat_rows = back_rows.reshape(experts_all * capacity, feature)
    picked = jnp.take(flat_rows, dest, axis=0).reshape(tok_rows, top, feature)
    input_grad = jnp.sum(picked.astype(jnp.float32), axis=1).astype(jnp.bfloat16)
    combine_grad = jnp.take(back_comb.reshape(-1), dest, axis=0).reshape(tok_rows, top)
    return (input_grad, combine_grad, gate_grad, up_grad, down_grad)


def solution(mesh):
    placed = (
        P(("dp", "expert"), None),
        P(("dp", "expert"), None),
        P(("dp", "expert"), None),
        P(("dp", "expert"), None),
        P("expert", None, None),
        P("expert", None, None),
        P("expert", None, None),
    )
    return jax.shard_map(
        shards,
        mesh=mesh,
        in_specs=placed,
        out_specs=(
            P(("dp", "expert"), None),
            P(("dp", "expert"), None),
            P("expert", "dp", None),
            P("expert", "dp", None),
            P("expert", "dp", None),
        ),
        check_vma=False,
    )
```

profile of v0, /device:TPU:0, one launch (start us, length us, event | category | flops | bytes accessed | tf_op | source)
XLA Modules:
  0.0 287.7 jit_solution(16933779392859275133)
XLA Ops:
  7.2 0.0 copy-start
  7.2 0.9 copy.30
  8.1 0.1 eq.26
  8.3 0.1 reshape.178
  8.4 0.8 copy.35
  9.2 0.1 reshape.180
  9.4 1.2 reduce-window.6
  10.6 0.1 slice.28
  10.7 0.1 copy.33
  10.8 0.1 copy.34
  10.9 0.1 add_bitcast_fusion
  11.0 0.1 mul.64
  11.2 1.4 scatter_custom_fusion
  12.6 3.4 %gather_fusion = bf16[512]{0:T(512)(128)(2,1)S(1)} fusion(bf16[256]{0:T(256)(128)(2,1)S(1)} %reshape.180, s32[1024]{0:T(1024)S(1)} %pad_clamp_fusion.2), kind=kCustom, calls=%fused_computation.2 | custom fusion | bytes 4096 | tf_op jit(solution)/shard_map/jit(_take)/gather | solution.py:31
  16.0 0.6 copy.36
  16.6 6.3 %all-to-all-start = ((bf16[4,1,128]{2,1,0:T(2,128)(2,1)}), bf16[4,1,128]{2,1,0:T(2,128)(2,1)S(1)}, u32[]{:S(2)}, u32[]{:S(2)}) async-start(bf16[4,1,128]{2,1,0:T(2,128)(2,1)} %copy.36), calls=%async_computation | async-start | bytes 4096 | tf_op jit(solution)/shard_map/all_to_all | solution.py:79
  23.0 6.3 %gather_fusion.4 = bf16[512,2048]{1,0:T(8,128)(2,1)} fusion(bf16[128,2048]{1,0:T(8,128)(2,1)} %param.9, s32[1024]{0:T(1024)S(1)} %pad_clamp_fusion.1), kind=kCustom, calls=%fused_computation.1.clone | custom fusion | bytes 4196352 | tf_op jit(solution)/shard_map/jit(_take)/gather | solution.py:26
  29.3 6.4 %gather_fusion.3 = bf16[512,2048]{1,0:T(8,128)(2,1)} fusion(bf16[128,2048]{1,0:T(8,128)(2,1)} %param.10, s32[1024]{0:T(1024)S(1)} %pad_clamp_fusion.1), kind=kCustom, calls=%fused_computation.clone | custom fusion | bytes 4196352 | tf_op jit(solution)/shard_map/jit(_take)/gather | solution.py:28
  35.7 4.0 %select_select_fusion.1 = (bf16[512,2048]{1,0:T(8,128)(2,1)}, bf16[512,2048]{1,0:T(8,128)(2,1)}) fusion(bf16[512,2048]{1,0:T(8,128)(2,1)} %gather_fusion.3, pred[512]{0:T(512)(128)(4,1)S(1)} %get-tuple-element.25, pred[512]{0:T(512)(128)(4,1)S(1)} %get-tuple-element.24, bf16[512,2048]{1,0:T(8,128)(2,1)} %gather_fusion.4), kind=kLoop, calls=%fused_computation.29 | loop fusion | flops 4194304 | bytes 8389632 | tf_op jit(solution)/shard_map/jit(_where)/select_n | solution.py:27
  39.6 0.0 all-to-all-done
  39.7 52.8 %all_to_all.22 = bf16[4,128,2048]{2,1,0:T(8,128)(2,1)} all-to-all(bf16[4,128,2048]{2,1,0:T(8,128)(2,1)} %bitcast.90), channel_id=1, replica_groups=mesh['dp'=8,'expert'=4] {'expert'}, dimensions={0} | all-to-all | bytes 4194304 | tf_op jit(solution)/shard_map/all_to_all | solution.py:77
  92.5 4.5 %all-to-all-start.1 = ((bf16[4,128,2048]{2,1,0:T(8,128)(2,1)}), bf16[4,128,2048]{2,1,0:T(8,128)(2,1)}, u32[]{:S(2)}, u32[]{:S(2)}) async-start(bf16[4,128,2048]{2,1,0:T(8,128)(2,1)} %bitcast.89), calls=%async_computation.1 | async-start | bytes 4194304 | tf_op jit(solution)/shard_map/all_to_all | solution.py:78
  96.9 0.2 reduce-scatter.3.cloned.1.call-start
  97.2 5.5 %fusion.5 = f32[512,768]{1,0:T(8,128)} fusion(bf16[512,2048]{1,0:T(8,128)(2,1)} %bitcast.91, bf16[1,2048,768]{2,1,0:T(8,128)(2,1)} %param.13), kind=kOutput, calls=%fused_computation.17 | convolution fusion | flops 1610612736 | bytes 6815744 | tf_op jit(solution)/shard_map/dot_general | solution.py:37
  102.7 41.5 %all-to-all-done.1 = bf16[4,128,2048]{2,1,0:T(8,128)(2,1)} async-done(((bf16[4,128,2048]{2,1,0:T(8,128)(2,1)}), bf16[4,128,2048]{2,1,0:T(8,128)(2,1)}, u32[]{:S(2)}, u32[]{:S(2)}) %all-to-all-start.1) | async-done | bytes 2097184 | tf_op jit(solution)/shard_map/all_to_all | solution.py:78
  144.2 2.1 fusion
  146.4 0.4 copy-done.2
  146.7 1.8 fusion.12
  148.6 0.0 copy-done
  148.6 0.2 copy-done.7
  148.8 3.2 %multiply_convert_fusion = (bf16[512,768]{1,0:T(8,128)(2,1)}, bf16[512,768]{1,0:T(8,128)(2,1)S(1)}, bf16[512,768]{1,0:T(8,128)(2,1)S(1)}) fusion(f32[512,768]{1,0:T(8,128)S(1)} %copy-done.7, f32[512,768]{1,0:T(8,128)S(1)} %fusion.12, bf16[512,2048]{1,0:T(8,128)(2,1)S(1)} %bitcast.92, bf16[1,2048,768]{2,1,0:T(8,128)(2,1)S(1)} %copy-done), kind=kOutput, calls=%fused_computation.34 | convolution fusion | flops 1616510976 | bytes 10747904 | tf_op jit(solution)/shard_map/dot_general | solution.py:38
  151.9 0.9 copy-done.3
  152.9 0.2 copy-done.5
  153.1 5.5 %convolution_convert_fusion = bf16[2048,1536]{1,0:T(8,128)(2,1)} fusion(bf16[512,2048]{1,0:T(8,128)(2,1)S(1)} %bitcast.93, bf16[512,768]{1,0:T(8,128)(2,1)S(1)} %get-tuple-element.29, bf16[512,768]{1,0:T(8,128)(2,1)S(1)} %get-tuple-element.28), kind=kOutput, calls=%fused_computation.6 | convolution fusion | flops 3227516928 | bytes 9961472 | tf_op jit(solution)/shard_map/dot_general | solution.py:94
  158.6 0.0 reduce-scatter.3.cloned.1.call-update
  158.7 4.7 %fusion.1 = bf16[512]{0:T(512)(128)(2,1)S(1)} fusion(bf16[4,128,2048]{2,1,0:T(8,128)(2,1)} %all-to-all-done.1, bf16[512,768]{1,0:T(8,128)(2,1)} %get-tuple-element.27, bf16[1,768,2048]{2,1,0:T(8,128)(2,1)} %param.15), kind=kOutput, calls=%fused_computation.11 | convolution fusion | flops 1613757952 | bytes 6030336 | tf_op jit(solution)/shard_map/dot_general | solution.py:42
  163.3 0.6 copy.38
  163.9 3.2 %all-to-all-start.4 = ((bf16[1,4,128]{2,0,1:T(2,128)(2,1)}), bf16[1,4,128]{2,0,1:T(2,128)(2,1)S(1)}, u32[]{:S(2)}, u32[]{:S(2)}) async-start(bf16[1,4,128]{2,0,1:T(2,128)(2,1)} %copy.38), calls=%async_computation.4 | async-start | bytes 4096 | tf_op jit(solution)/shard_map/all_to_all | solution.py:121
  167.2 0.3 reduce-scatter.5.cloned.1.call-start
  167.4 0.0 copy-start.6
  167.4 2.4 fusion.2
  169.8 0.0 copy-done.6
  169.8 3.6 %convolution_convert_fusion.1 = bf16[768,2048]{1,0:T(8,128)(2,1)} fusion(bf16[512,768]{1,0:T(8,128)(2,1)S(1)} %copy-done.6, bf16[512,2048]{1,0:T(8,128)(2,1)S(1)} %fusion.2), kind=kOutput, calls=%fused_computation.14 | convolution fusion | flops 1612185600 | bytes 6029312 | tf_op jit(solution)/shard_map/dot_general | solution.py:97
  173.4 0.0 reduce-scatter.5.cloned.1.call-update
  173.5 0.0 copy-start.4
  173.5 4.1 %fusion.3 = f32[512,2048]{1,0:T(8,128)S(1)} fusion(bf16[512,768]{1,0:T(8,128)(2,1)} %copy-done.5, bf16[1,2048,768]{2,1,0:T(8,128)(2,1)} %param.13), kind=kOutput, calls=%fused_computation.15 | convolution fusion | flops 1610612736 | bytes 8126464 | tf_op jit(solution)/shard_map/dot_general | solution.py:54
  177.5 1.8 fusion.16
  179.4 5.3 %copy.46 = bf16[1,512,2048]{2,0,1:T(2,128)(2,1)} copy(bf16[1,512,2048]{2,1,0:T(8,128)(2,1)S(1)} %fusion.16) | data formatting | bytes 4194304 | tf_op jit(solution)/shard_map/stack | solution.py:120
  184.6 0.5 broadcast.139
  185.1 14.5 %reduce.1 = bf16[512,2048]{1,0:T(8,128)(2,1)} reduce(bf16[512,1,2048]{2,1,0:T(2,128)(2,1)} %bitcast.87, bf16[]{:T(256)} %broadcast.139), dimensions={1}, to_apply=%bitcast.83.reduce_sub_computation | reduce | bytes 4194306
  199.6 4.6 %reshape.245 = bf16[4,2,131072]{2,1,0:T(2,128)(2,1)} reshape(bf16[512,2048]{1,0:T(8,128)(2,1)} %reduce.1) | data formatting | bytes 4194304
  204.2 0.0 all-to-all-done.4
  204.2 4.8 %all-to-all-start.3 = ((bf16[4,2,131072]{2,1,0:T(2,128)(2,1)}), bf16[4,2,131072]{2,1,0:T(2,128)(2,1)}, u32[]{:S(2)}, u32[]{:S(2)}) async-start(bf16[4,2,131072]{2,1,0:T(2,128)(2,1)} %reshape.245), calls=%async_computation.3 | async-start | bytes 4194304 | tf_op jit(solution)/shard_map/all_to_all | solution.py:120
  209.0 0.1 reduce_sum.35
  209.2 1.9 gather_fusion.2
  211.1 0.1 gather.23
  211.3 0.6 copy.39
  211.9 44.8 %all-to-all-done.3 = bf16[4,2,131072]{2,1,0:T(2,128)(2,1)} async-done(((bf16[4,2,131072]{2,1,0:T(2,128)(2,1)}), bf16[4,2,131072]{2,1,0:T(2,128)(2,1)}, u32[]{:S(2)}, u32[]{:S(2)}) %all-to-all-start.3) | async-done | bytes 2097184 | tf_op jit(solution)/shard_map/all_to_all | solution.py:120
  256.8 5.0 %reshape.246 = bf16[512,1,2048]{2,1,0:T(2,128)(2,1)} reshape(bf16[4,2,131072]{2,1,0:T(2,128)(2,1)} %all-to-all-done.3) | data formatting | bytes 4194304
  261.7 4.9 %copy.45 = bf16[1,512,2048]{2,1,0:T(8,128)(2,1)} copy(bf16[1,512,2048]{2,0,1:T(2,128)(2,1)} %bitcast.88) | data formatting | bytes 4194304
  266.6 5.2 %gather_fusion.1 = bf16[256,2048]{1,0:T(8,128)(2,1)} fusion(bf16[512,2048]{1,0:T(8,128)(2,1)} %bitcast.86, s32[1024]{0:T(1024)S(1)} %pad_clamp_fusion), kind=kCustom, calls=%fused_computation.3 | custom fusion | bytes 2098176 | tf_op jit(solution)/shard_map/jit(_take)/gather | solution.py:130
  271.9 2.6 gather.21
  274.4 4.4 %fusion.23 = bf16[128,2048]{1,0:T(8,128)(2,1)} fusion(bf16[128,2,2048]{2,1,0:T(2,128)(2,1)} %gather.21, pred[128,2]{1,0:T(8,128)(4,1)S(1)} %get-tuple-element.22), kind=kLoop, calls=%fused_computation.39 | loop fusion | flops 786432 | bytes 1573120 | tf_op jit(solution)/shard_map/reduce_sum | solution.py:131
  278.8 2.0 slice_bitcast_fusion
  (25 shorter events, 0.2 us)
Async XLA Ops:
  7.2 141.4 %copy-start = (bf16[1,2048,768]{2,1,0:T(8,128)(2,1)S(1)}, bf16[1,2048,768]{2,1,0:T(8,128)(2,1)}, u32[]{:S(2)}) copy-start(bf16[1,2048,768]{2,1,0:T(8,128)(2,1)} %param.14) | copy-start | bytes 9437188
  16.6 23.1 %all-to-all-start = ((bf16[4,1,128]{2,1,0:T(2,128)(2,1)}), bf16[4,1,128]{2,1,0:T(2,128)(2,1)S(1)}, u32[]{:S(2)}, u32[]{:S(2)}) async-start(bf16[4,1,128]{2,1,0:T(2,128)(2,1)} %copy.36), calls=%async_computation | async-start | bytes 4096 | tf_op jit(solution)/shard_map/all_to_all | solution.py:79
  92.5 51.7 %all-to-all-start.1 = ((bf16[4,128,2048]{2,1,0:T(8,128)(2,1)}), bf16[4,128,2048]{2,1,0:T(8,128)(2,1)}, u32[]{:S(2)}, u32[]{:S(2)}) async-start(bf16[4,128,2048]{2,1,0:T(8,128)(2,1)} %bitcast.89), calls=%async_computation.1 | async-start | bytes 4194304 | tf_op jit(solution)/shard_map/all_to_all | solution.py:78
  96.9 181.9 %reduce-scatter.3.cloned.1.call-start = ((), (), s32[]{:S(2)}) async-start(), calls=%async_computation.7 | async-start | bytes 7077888 | tf_op jit(solution)/shard_map/reduce_scatter | solution.py:99
  144.2 2.5 copy-start.2
  146.7 1.9 copy-start.1
  146.7 2.0 copy-start.7
  151.9 0.9 copy-start.3
  151.9 1.2 copy-start.5
  163.9 40.2 %all-to-all-start.4 = ((bf16[1,4,128]{2,0,1:T(2,128)(2,1)}), bf16[1,4,128]{2,0,1:T(2,128)(2,1)S(1)}, u32[]{:S(2)}, u32[]{:S(2)}) async-start(bf16[1,4,128]{2,0,1:T(2,128)(2,1)} %copy.38), calls=%async_computation.4 | async-start | bytes 4096 | tf_op jit(solution)/shard_map/all_to_all | solution.py:121
  167.2 113.7 %reduce-scatter.5.cloned.1.call-start = ((), (), s32[]{:S(2)}) async-start(), calls=%async_computation.8 | async-start | bytes 3538944 | tf_op jit(solution)/shard_map/reduce_scatter | solution.py:107
  167.4 2.4 copy-start.6
  173.5 4.1 %copy-start.4 = (bf16[512,768]{1,0:T(8,128)(2,1)S(1)}, bf16[512,768]{1,0:T(8,128)(2,1)}, u32[]{:S(2)}) copy-start(bf16[512,768]{1,0:T(8,128)(2,1)} %copy-done.3) | copy-start | bytes 2359300
  204.2 52.6 %all-to-all-start.3 = ((bf16[4,2,131072]{2,1,0:T(2,128)(2,1)}), bf16[4,2,131072]{2,1,0:T(2,128)(2,1)}, u32[]{:S(2)}, u32[]{:S(2)}) async-start(bf16[4,2,131072]{2,1,0:T(2,128)(2,1)} %reshape.245), calls=%async_computation.3 | async-start | bytes 4194304 | tf_op jit(solution)/shard_map/all_to_all | solution.py:120
Sparse Core Ops, SparseCore 0:
  158.8 60.8 reduce-scatter.2
  223.6 46.0 reduce-scatter.4
where the time goes:
time: 289 us; the launch traced here: 288 us
  waiting for transfers between devices  86.4 us (30%)
  local copies, waits for them, and re-layouts  55.8 us (19%)
  blocking collectives  52.8 us (18%)
  matrix products  30.2 us (10%)
  other arithmetic  28.8 us (10%)
  starting transfers between devices  19.3 us (7%)
  between operations  14.3 us (5%)
    all_to_all x1, blocking collectives, shards(): lax.all_to_all(rows_x, 'expert', split_axis=0, concat_axis=1, tiled=True)  52.8 us
    all_to_all x1, waiting for transfers between devices, shards(): lax.all_to_all(jnp.stack(row_list), 'expert', split_axis=1, concat_axis=0...  44.8 us
    all_to_all x1, waiting for transfers between devices, shards(): lax.all_to_all(rows_dy, 'expert', split_axis=0, concat_axis=1, tiled=True)  41.5 us
    unnamed x23, local copies, waits for them, and re-layouts  19 us
    unnamed x2, other arithmetic  14.5 us
    gather x2, local copies, waits for them, and re-layouts, shards(): picked = jnp.take(flat_rows, dest, axis=0).reshape(tok_rows, top, feature)  7.81 us
    gather x1, local copies, waits for them, and re-layouts, gather_rows(): jnp.take(cotangent, source, axis=0)  6.36 us
    all_to_all x1, starting transfers between devices, shards(): lax.all_to_all(rows_c.astype(jnp.bfloat16), 'expert', split_axis=0, conca...  6.35 us
  transfers between devices with their start and end apart: 6, of which 2 were waited for; matrix products, arithmetic and copies ran while one was open for 32% of the time, Pallas kernels for 0%

commit v1 on v0

--- a/solution.py
+++ b/solution.py
@@ -2,6 +2,29 @@
 import jax.numpy as jnp
 from jax import lax
 from jax.sharding import PartitionSpec as P
+
+
+def cut_along(x, dim, size):
+    shape = x.shape
+    blocks = x.reshape(*shape[:dim], size, shape[dim] // size, *shape[dim + 1 :])
+    return jnp.moveaxis(blocks, dim, 0)
+
+
+def laid_out(tiles, dim):
+    tiles = jnp.moveaxis(tiles, 0, dim)
+    shape = tiles.shape
+    return tiles.reshape(*shape[:dim], shape[dim] * shape[dim + 1], *shape[dim + 2 :])
+
+
+def pairwise_exchange(shard, axis, split_dim, concat_dim):
+    size, index = (lax.axis_size(axis), lax.axis_index(axis))
+    blocks = cut_along(shard, split_dim, size)
+    gathered = [blocks[index]]
+    for step in range(1, size):
+        sent = blocks[index ^ step]
+        gathered.append(lax.ppermute(sent, axis, [(i, i ^ step) for i in range(size)]))
+    blocks = jnp.stack(gathered)[index ^ jnp.arange(size)]
+    return laid_out(blocks, concat_dim)
 
 
 def slot_table(expert_ids, experts_all, capacity):
@@ -74,7 +97,7 @@
     rows_dy = rows_dy.reshape(experts_all, capacity, feature)
     rows_c = rows_c.reshape(experts_all, capacity)
     recv_x, recv_dy, recv_c = (
-        lax.all_to_all(rows_x, "expert", split_axis=0, concat_axis=1, tiled=True),
+        pairwise_exchange(rows_x, "expert", 0, 1),
         lax.all_to_all(rows_dy, "expert", split_axis=0, concat_axis=1, tiled=True),
         lax.all_to_all(
             rows_c.astype(jnp.bfloat16), "expert", split_axis=0, concat_axis=1, tiled=True

time: 289 us -> 292 us (1.010)
  blocking collectives: 52.8 us -> 0 us
  waiting for transfers between devices: 86.4 us -> 131 us
  local copies, waits for them, and re-layouts: 55.8 us -> 61.1 us
  starting transfers between devices: 19.3 us -> 24.3 us
    ppermute x0 -> x3, waiting for transfers between devices: none -> 86.3 us  [pairwise_exchange(): lax.ppermute(sent, axis, [(i, i ^ step) for i in range(size)])]
    all_to_all x1 -> x0, blocking collectives: 52.8 us -> none  [shards(): lax.all_to_all(rows_x, 'expert', split_axis=0, concat_axis=1, tiled=True)]
    all_to_all x1, waiting for transfers between devices: 41.5 us -> 0.01 us  [shards(): lax.all_to_all(rows_dy, 'expert', split_axis=0, concat_axis=1, tiled=True)]
    ppermute x0 -> x3, starting transfers between devices: none -> 4.53 us  [pairwise_exchange(): lax.ppermute(sent, axis, [(i, i ^ step) for i in range(size)])]
    gather x0 -> x1, local copies, waits for them, and re-layouts: none -> 3.58 us  [pairwise_exchange(): blocks = jnp.stack(gathered)[index ^ jnp.arange(size)]]
  transfers between devices with their start and end apart: 6 -> 9, of which waited for: 2 -> 3; matrix products, arithmetic and copies ran while one was open for 32% -> 34% of each run, Pallas kernels for 0% -> 0%
where the time goes in v1:
time: 292 us; the launch traced here: 291 us
  waiting for transfers between devices  131 us (45%)
  local copies, waits for them, and re-layouts  61.1 us (21%)
  other arithmetic  30.3 us (10%)
  matrix products  30.2 us (10%)
  starting transfers between devices  24.3 us (8%)
  between operations  14.3 us (5%)
    ppermute x3, waiting for transfers between devices, pairwise_exchange(): lax.ppermute(sent, axis, [(i, i ^ step) for i in range(size)])  86.3 us
    all_to_all x1, waiting for transfers between devices, shards(): lax.all_to_all(jnp.stack(row_list), 'expert', split_axis=1, concat_axis=0...  44.8 us
    unnamed x23, local copies, waits for them, and re-layouts  19 us
    unnamed x2, other arithmetic  14.5 us
    gather x2, local copies, waits for them, and re-layouts, shards(): picked = jnp.take(flat_rows, dest, axis=0).reshape(tok_rows, top, feature)  7.81 us
    gather x1, local copies, waits for them, and re-layouts, gather_rows(): jnp.take(tokens, source, axis=0)  6.4 us
    gather x1, local copies, waits for them, and re-layouts, gather_rows(): jnp.take(cotangent, source, axis=0)  6.35 us
    all_to_all x1, starting transfers between devices, shards(): lax.all_to_all(rows_c.astype(jnp.bfloat16), 'expert', split_axis=0, conca...  6.35 us
  transfers between devices with their start and end apart: 9, of which 3 were waited for; matrix products, arithmetic and copies ran while one was open for 34% of the time, Pallas kernels for 0%

profile of v1, /device:TPU:0, one launch (start us, length us, event | category | flops | bytes accessed | tf_op | source)
XLA Modules:
  0.0 291.5 jit_solution(647359564526285780)
XLA Ops:
  7.2 0.0 copy-start
  7.2 0.9 copy.30
  8.1 0.1 eq.26
  8.3 0.1 reshape.187
  8.4 0.8 copy.35
  9.2 0.1 reshape.189
  9.4 1.2 reduce-window.6
  10.6 0.1 slice.30
  10.7 0.1 copy.33
  10.8 0.1 copy.34
  10.9 0.1 add_bitcast_fusion
  11.0 0.1 mul.64
  11.2 1.4 scatter_custom_fusion
  12.6 3.4 %gather_fusion = bf16[512]{0:T(512)(128)(2,1)S(1)} fusion(bf16[256]{0:T(256)(128)(2,1)S(1)} %reshape.189, s32[1024]{0:T(1024)S(1)} %pad_clamp_fusion.3), kind=kCustom, calls=%fused_computation.2 | custom fusion | bytes 4096 | tf_op jit(solution)/shard_map/jit(_take)/gather | solution.py:54
  16.0 0.6 copy.36
  16.6 6.3 %all-to-all-start = ((bf16[4,1,128]{2,1,0:T(2,128)(2,1)}), bf16[4,1,128]{2,1,0:T(2,128)(2,1)S(1)}, u32[]{:S(2)}, u32[]{:S(2)}) async-start(bf16[4,1,128]{2,1,0:T(2,128)(2,1)} %copy.36), calls=%async_computation | async-start | bytes 4096 | tf_op jit(solution)/shard_map/all_to_all | solution.py:102
  23.0 6.4 %gather_fusion.5 = bf16[512,2048]{1,0:T(8,128)(2,1)} fusion(bf16[128,2048]{1,0:T(8,128)(2,1)} %param.9, s32[1024]{0:T(1024)S(1)} %pad_clamp_fusion.2), kind=kCustom, calls=%fused_computation.1.clone | custom fusion | bytes 4196352 | tf_op jit(solution)/shard_map/jit(_take)/gather | solution.py:49
  29.4 6.4 %gather_fusion.4 = bf16[512,2048]{1,0:T(8,128)(2,1)} fusion(bf16[128,2048]{1,0:T(8,128)(2,1)} %param.10, s32[1024]{0:T(1024)S(1)} %pad_clamp_fusion.2), kind=kCustom, calls=%fused_computation.clone | custom fusion | bytes 4196352 | tf_op jit(solution)/shard_map/jit(_take)/gather | solution.py:51
  35.7 3.9 %select_select_fusion.1 = (bf16[512,2048]{1,0:T(8,128)(2,1)}, bf16[512,2048]{1,0:T(8,128)(2,1)}) fusion(bf16[512,2048]{1,0:T(8,128)(2,1)} %gather_fusion.4, pred[512]{0:T(512)(128)(4,1)S(1)} %get-tuple-element.25, pred[512]{0:T(512)(128)(4,1)S(1)} %get-tuple-element.24, bf16[512,2048]{1,0:T(8,128)(2,1)} %gather_fusion.5), kind=kLoop, calls=%fused_computation.31 | loop fusion | flops 4194304 | bytes 8389632 | tf_op jit(solution)/shard_map/jit(_where)/select_n | solution.py:50
  39.6 5.1 %all-to-all-start.1 = ((bf16[4,128,2048]{2,1,0:T(8,128)(2,1)}), bf16[4,128,2048]{2,1,0:T(8,128)(2,1)}, u32[]{:S(2)}, u32[]{:S(2)}) async-start(bf16[4,128,2048]{2,1,0:T(8,128)(2,1)} %bitcast.102), calls=%async_computation.1 | async-start | bytes 4194304 | tf_op jit(solution)/shard_map/all_to_all | solution.py:101
  44.7 0.0 reduce-scatter.3.cloned.1.call-start
  44.7 1.7 constant_dynamic-slice_fusion
  46.4 3.9 %collective-permute-start.2 = (bf16[1,128,2048]{2,1,0:T(8,128)(2,1)S(1)}, bf16[1,128,2048]{2,1,0:T(8,128)(2,1)S(1)}, u32[]{:S(2)}, u32[]{:S(2)}) collective-permute-start(bf16[1,128,2048]{2,1,0:T(8,128)(2,1)S(1)} %get-tuple-element.31), channel_id=1, source_target_pairs={{0,3},{1,2},{2,1},{3,0},{4,7},{5,6},{6,5},{7,4},{8,11},{9,10},{10,... | collective-permute-start | bytes 1572872 | tf_op jit(solution)/shard_map/ppermute | solution.py:25
  50.3 0.6 collective-permute-start
  50.9 44.4 %collective-permute-done.2 = bf16[1,128,2048]{2,1,0:T(8,128)(2,1)S(1)} collective-permute-done((bf16[1,128,2048]{2,1,0:T(8,128)(2,1)S(1)}, bf16[1,128,2048]{2,1,0:T(8,128)(2,1)S(1)}, u32[]{:S(2)}, u32[]{:S(2)}) %collective-permute-start.2) | collective-permute-done | bytes 524320 | tf_op jit(solution)/shard_map/ppermute | solution.py:25
  95.3 42.0 %collective-permute-done.1 = bf16[1,128,2048]{2,1,0:T(8,128)(2,1)S(1)} collective-permute-done((bf16[1,128,2048]{2,1,0:T(8,128)(2,1)S(1)}, bf16[1,128,2048]{2,1,0:T(8,128)(2,1)S(1)}, u32[]{:S(2)}, u32[]{:S(2)}) %collective-permute-start.1) | collective-permute-done | bytes 524320 | tf_op jit(solution)/shard_map/ppermute | solution.py:25
  137.3 1.6 maximum_bitcast_fusion
  138.9 3.6 %gather_fusion.1 = bf16[4,128,2048]{2,1,0:T(8,128)(2,1)} fusion(bf16[4,128,2048]{2,1,0:T(8,128)(2,1)} %maximum_bitcast_fusion, s32[1024]{0:T(1024)S(1)} %pad_clamp_fusion.1), kind=kCustom, calls=%fused_computation.3 | custom fusion | bytes 4194320 | tf_op jit(solution)/shard_map/gather | solution.py:26
  142.5 5.5 %fusion.5 = f32[512,768]{1,0:T(8,128)} fusion(bf16[512,2048]{1,0:T(8,128)(2,1)} %bitcast.104, bf16[1,2048,768]{2,1,0:T(8,128)(2,1)} %param.13), kind=kOutput, calls=%fused_computation.18 | convolution fusion | flops 1610612736 | bytes 6815744 | tf_op jit(solution)/shard_map/dot_general | solution.py:60
  147.9 0.0 all-to-all-done.1
  147.9 2.1 fusion
  150.1 0.4 copy-done.2
  150.5 1.8 fusion.12
  152.3 0.2 copy-done.7
  152.5 3.1 %multiply_convert_fusion = (bf16[512,768]{1,0:T(8,128)(2,1)}, bf16[512,768]{1,0:T(8,128)(2,1)S(1)}, bf16[512,768]{1,0:T(8,128)(2,1)S(1)}) fusion(f32[512,768]{1,0:T(8,128)S(1)} %copy-done.7, f32[512,768]{1,0:T(8,128)S(1)} %fusion.12, bf16[512,2048]{1,0:T(8,128)(2,1)S(1)} %bitcast.105, bf16[1,2048,768]{2,1,0:T(8,128)(2,1)S(1)} %copy-done), kind=kOutput, calls=%fused_computation.36 | convolution fusion | flops 1616510976 | bytes 10747904 | tf_op jit(solution)/shard_map/dot_general | solution.py:61
  155.6 0.9 copy-done.3
  156.6 0.2 copy-done.5
  156.8 5.6 %convolution_convert_fusion = bf16[2048,1536]{1,0:T(8,128)(2,1)} fusion(bf16[512,2048]{1,0:T(8,128)(2,1)S(1)} %bitcast.106, bf16[512,768]{1,0:T(8,128)(2,1)S(1)} %get-tuple-element.29, bf16[512,768]{1,0:T(8,128)(2,1)S(1)} %get-tuple-element.28), kind=kOutput, calls=%fused_computation.7 | convolution fusion | flops 3227516928 | bytes 9961472 | tf_op jit(solution)/shard_map/dot_general | solution.py:117
  162.4 0.0 reduce-scatter.3.cloned.1.call-update
  162.4 4.7 %fusion.1 = bf16[512]{0:T(512)(128)(2,1)S(1)} fusion(bf16[4,128,2048]{2,1,0:T(8,128)(2,1)} %all-to-all-done.1, bf16[512,768]{1,0:T(8,128)(2,1)} %get-tuple-element.27, bf16[1,768,2048]{2,1,0:T(8,128)(2,1)} %param.15), kind=kOutput, calls=%fused_computation.12 | convolution fusion | flops 1613757952 | bytes 6030336 | tf_op jit(solution)/shard_map/dot_general | solution.py:65
  167.1 0.6 copy.38
  167.7 3.2 %all-to-all-start.3 = ((bf16[1,4,128]{2,0,1:T(2,128)(2,1)}), bf16[1,4,128]{2,0,1:T(2,128)(2,1)S(1)}, u32[]{:S(2)}, u32[]{:S(2)}) async-start(bf16[1,4,128]{2,0,1:T(2,128)(2,1)} %copy.38), calls=%async_computation.3 | async-start | bytes 4096 | tf_op jit(solution)/shard_map/all_to_all | solution.py:144
  170.9 0.3 reduce-scatter.5.cloned.1.call-start
  171.2 2.4 fusion.2
  173.6 3.6 %convolution_convert_fusion.1 = bf16[768,2048]{1,0:T(8,128)(2,1)} fusion(bf16[512,768]{1,0:T(8,128)(2,1)S(1)} %copy-done.6, bf16[512,2048]{1,0:T(8,128)(2,1)S(1)} %fusion.2), kind=kOutput, calls=%fused_computation.15 | convolution fusion | flops 1612185600 | bytes 6029312 | tf_op jit(solution)/shard_map/dot_general | solution.py:120
  177.2 0.0 reduce-scatter.5.cloned.1.call-update
  177.2 4.1 %fusion.3 = f32[512,2048]{1,0:T(8,128)S(1)} fusion(bf16[512,768]{1,0:T(8,128)(2,1)} %copy-done.5, bf16[1,2048,768]{2,1,0:T(8,128)(2,1)} %param.13), kind=kOutput, calls=%fused_computation.16 | convolution fusion | flops 1610612736 | bytes 8126464 | tf_op jit(solution)/shard_map/dot_general | solution.py:77
  181.3 1.8 fusion.16
  183.1 5.3 %copy.46 = bf16[1,512,2048]{2,0,1:T(2,128)(2,1)} copy(bf16[1,512,2048]{2,1,0:T(8,128)(2,1)S(1)} %fusion.16) | data formatting | bytes 4194304 | tf_op jit(solution)/shard_map/stack | solution.py:143
  188.4 0.5 broadcast.174
  188.9 14.5 %reduce.1 = bf16[512,2048]{1,0:T(8,128)(2,1)} reduce(bf16[512,1,2048]{2,1,0:T(2,128)(2,1)} %bitcast.100, bf16[]{:T(256)} %broadcast.174), dimensions={1}, to_apply=%bitcast.96.reduce_sub_computation | reduce | bytes 4194306
  203.4 4.6 %reshape.264 = bf16[4,2,131072]{2,1,0:T(2,128)(2,1)} reshape(bf16[512,2048]{1,0:T(8,128)(2,1)} %reduce.1) | data formatting | bytes 4194304
  208.0 4.8 %all-to-all-start.2 = ((bf16[4,2,131072]{2,1,0:T(2,128)(2,1)}), bf16[4,2,131072]{2,1,0:T(2,128)(2,1)}, u32[]{:S(2)}, u32[]{:S(2)}) async-start(bf16[4,2,131072]{2,1,0:T(2,128)(2,1)} %reshape.264), calls=%async_computation.2 | async-start | bytes 4194304 | tf_op jit(solution)/shard_map/all_to_all | solution.py:143
  212.8 0.1 reduce_sum.35
  212.9 1.9 gather_fusion.3
  214.9 0.1 gather.27
  215.1 0.6 copy.39
  215.7 44.8 %all-to-all-done.2 = bf16[4,2,131072]{2,1,0:T(2,128)(2,1)} async-done(((bf16[4,2,131072]{2,1,0:T(2,128)(2,1)}), bf16[4,2,131072]{2,1,0:T(2,128)(2,1)}, u32[]{:S(2)}, u32[]{:S(2)}) %all-to-all-start.2) | async-done | bytes 2097184 | tf_op jit(solution)/shard_map/all_to_all | solution.py:143
  260.5 5.0 %reshape.265 = bf16[512,1,2048]{2,1,0:T(2,128)(2,1)} reshape(bf16[4,2,131072]{2,1,0:T(2,128)(2,1)} %all-to-all-done.2) | data formatting | bytes 4194304
  265.5 4.9 %copy.45 = bf16[1,512,2048]{2,1,0:T(8,128)(2,1)} copy(bf16[1,512,2048]{2,0,1:T(2,128)(2,1)} %bitcast.101) | data formatting | bytes 4194304
  270.4 5.2 %gather_fusion.2 = bf16[256,2048]{1,0:T(8,128)(2,1)} fusion(bf16[512,2048]{1,0:T(8,128)(2,1)} %bitcast.99, s32[1024]{0:T(1024)S(1)} %pad_clamp_fusion), kind=kCustom, calls=%fused_computation.4 | custom fusion | bytes 2098176 | tf_op jit(solution)/shard_map/jit(_take)/gather | solution.py:153
  275.6 2.6 gather.25
  278.2 4.4 %fusion.23 = bf16[128,2048]{1,0:T(8,128)(2,1)} fusion(bf16[128,2,2048]{2,1,0:T(2,128)(2,1)} %gather.25, pred[128,2]{1,0:T(8,128)(4,1)S(1)} %get-tuple-element.22), kind=kLoop, calls=%fused_computation.41 | loop fusion | flops 786432 | bytes 1573120 | tf_op jit(solution)/shard_map/reduce_sum | solution.py:154
  282.6 2.0 slice_bitcast_fusion
  (35 shorter events, 0.2 us)
Async XLA Ops:
  7.2 145.1 %copy-start = (bf16[1,2048,768]{2,1,0:T(8,128)(2,1)S(1)}, bf16[1,2048,768]{2,1,0:T(8,128)(2,1)}, u32[]{:S(2)}) copy-start(bf16[1,2048,768]{2,1,0:T(8,128)(2,1)} %param.14) | copy-start | bytes 9437188
  16.6 23.0 %all-to-all-start = ((bf16[4,1,128]{2,1,0:T(2,128)(2,1)}), bf16[4,1,128]{2,1,0:T(2,128)(2,1)S(1)}, u32[]{:S(2)}, u32[]{:S(2)}) async-start(bf16[4,1,128]{2,1,0:T(2,128)(2,1)} %copy.36), calls=%async_computation | async-start | bytes 4096 | tf_op jit(solution)/shard_map/all_to_all | solution.py:102
  39.6 108.3 %all-to-all-start.1 = ((bf16[4,128,2048]{2,1,0:T(8,128)(2,1)}), bf16[4,128,2048]{2,1,0:T(8,128)(2,1)}, u32[]{:S(2)}, u32[]{:S(2)}) async-start(bf16[4,128,2048]{2,1,0:T(8,128)(2,1)} %bitcast.102), calls=%async_computation.1 | async-start | bytes 4194304 | tf_op jit(solution)/shard_map/all_to_all | solution.py:101
  44.7 237.9 %reduce-scatter.3.cloned.1.call-start = ((), (), s32[]{:S(2)}) async-start(), calls=%async_computation.6 | async-start | bytes 7077888 | tf_op jit(solution)/shard_map/reduce_scatter | solution.py:122
  46.4 48.9 %collective-permute-start.2 = (bf16[1,128,2048]{2,1,0:T(8,128)(2,1)S(1)}, bf16[1,128,2048]{2,1,0:T(8,128)(2,1)S(1)}, u32[]{:S(2)}, u32[]{:S(2)}) collective-permute-start(bf16[1,128,2048]{2,1,0:T(8,128)(2,1)S(1)} %get-tuple-element.31), channel_id=1, source_target_pairs={{0,3},{1,2},{2,1},{3,0},{4,7},{5,6},{6,5},{7,4},{8,11},{9,10},{10,... | collective-permute-start | bytes 1572872 | tf_op jit(solution)/shard_map/ppermute | solution.py:25
  50.3 87.0 %collective-permute-start.1 = (bf16[1,128,2048]{2,1,0:T(8,128)(2,1)S(1)}, bf16[1,128,2048]{2,1,0:T(8,128)(2,1)S(1)}, u32[]{:S(2)}, u32[]{:S(2)}) collective-permute-start(bf16[1,128,2048]{2,1,0:T(8,128)(2,1)S(1)} %get-tuple-element.32), channel_id=1, source_target_pairs={{0,2},{1,3},{2,0},{3,1},{4,6},{5,7},{6,4},{7,5},{8,10},{9,11},{10,... | collective-permute-start | bytes 1572872 | tf_op jit(solution)/shard_map/ppermute | solution.py:25
  50.3 87.0 %collective-permute-start = (bf16[1,128,2048]{2,1,0:T(8,128)(2,1)S(1)}, bf16[1,128,2048]{2,1,0:T(8,128)(2,1)S(1)}, u32[]{:S(2)}, u32[]{:S(2)}) collective-permute-start(bf16[1,128,2048]{2,1,0:T(8,128)(2,1)S(1)} %get-tuple-element.33), channel_id=1, source_target_pairs={{0,1},{1,0},{2,3},{3,2},{4,5},{5,4},{6,7},{7,6},{8,9},{9,8},{10,11... | collective-permute-start | bytes 1572872 | tf_op jit(solution)/shard_map/ppermute | solution.py:25
  147.9 2.5 copy-start.2
  150.5 1.9 copy-start.1
  150.5 2.0 copy-start.7
  155.6 0.9 copy-start.3
  155.6 1.2 copy-start.5
  167.7 40.3 %all-to-all-start.3 = ((bf16[1,4,128]{2,0,1:T(2,128)(2,1)}), bf16[1,4,128]{2,0,1:T(2,128)(2,1)S(1)}, u32[]{:S(2)}, u32[]{:S(2)}) async-start(bf16[1,4,128]{2,0,1:T(2,128)(2,1)} %copy.38), calls=%async_computation.3 | async-start | bytes 4096 | tf_op jit(solution)/shard_map/all_to_all | solution.py:144
  170.9 113.7 %reduce-scatter.5.cloned.1.call-start = ((), (), s32[]{:S(2)}) async-start(), calls=%async_computation.7 | async-start | bytes 3538944 | tf_op jit(solution)/shard_map/reduce_scatter | solution.py:130
  171.2 2.4 copy-start.6
  177.2 4.1 %copy-start.4 = (bf16[512,768]{1,0:T(8,128)(2,1)S(1)}, bf16[512,768]{1,0:T(8,128)(2,1)}, u32[]{:S(2)}) copy-start(bf16[512,768]{1,0:T(8,128)(2,1)} %copy-done.3) | copy-start | bytes 2359300
  208.0 52.6 %all-to-all-start.2 = ((bf16[4,2,131072]{2,1,0:T(2,128)(2,1)}), bf16[4,2,131072]{2,1,0:T(2,128)(2,1)}, u32[]{:S(2)}, u32[]{:S(2)}) async-start(bf16[4,2,131072]{2,1,0:T(2,128)(2,1)} %reshape.264), calls=%async_computation.2 | async-start | bytes 4194304 | tf_op jit(solution)/shard_map/all_to_all | solution.py:143
Sparse Core Ops, SparseCore 0:
  162.5 60.8 reduce-scatter.2
  227.4 46.0 reduce-scatter.4
